TPU v7x, 32 devices: a whole 2x2x4 slice. The times are simulated.
32 devices in a mesh: grid: 8 (over y, x, core), band: 4 (over z).
Axes of the slice: x: 2, y: 2, z: 4, core: 2. Of those that a mesh axis runs over, the one named last changes fastest.
Arguments:
- start: float32 [1, 4, 1, 64, 32768], P(None, None, None, 'band', 'grid'), may hold values from -6 to 6
- energies: float32 [4, 64, 32768], P(None, 'band', 'grid'), may hold values from -4 to 4
- sites: int32 [3, 1], replicated, may hold values from 0 to 31
- potential: float32 [32, 32, 32], replicated, may hold values from -4 to 400
Outputs:
- alphas: float32 [1, 1, 4], replicated
- betas: float32 [1, 1, 4], replicated
- lanczos: float32 [1, 4, 1, 64, 32768], P(None, None, None, 'band', 'grid')
All inputs are finite; a program needn't handle non-finite values.
Results may differ from a plain program's by a relative error of at most 0.0003.
Values sent between devices are 32-bit elements; how exact they have to be, the bound alone decides.
No kernel may reach another device: no remote copies, remote signals or barrier semaphores. Data moves between devices by JAX's collectives and lax.ppermute only.
A program may use at most 64 MiB of HBM per device.

v0:
```python
import math

import jax
import jax.numpy as jnp
from jax import lax
from jax.sharding import PartitionSpec as P

ITERS = 4


precise_mode = lax.Precision.HIGHEST


def cas_table(grid_size):
    cells = jnp.arange(grid_size, dtype=jnp.int32)
    phase = cells[:, None] * cells[None, :] % grid_size
    angle = phase.astype(jnp.float32) * (2.0 * math.pi / grid_size)
    return jnp.cos(angle) + jnp.sin(angle)


def shift_axis(field_part, offset, axis_number):
    length = field_part.shape[axis_number]
    doubled = jnp.concatenate([field_part, field_part], axis=axis_number)
    first_index = (length - offset) % length
    return lax.dynamic_slice_in_dim(doubled, first_index, length, axis_number)


def expand_coef(values):
    return values[:, None, :, None, None]


def body(start, energies, sites, potential):
    grid_size = potential.shape[0]
    volume = grid_size * grid_size * grid_size
    atom_count, core_count, pol_count, band_local, kpoint_local = start.shape
    plane_count = grid_size // lax.axis_size("grid")
    position = lax.axis_index("grid")
    chain_count = core_count * pol_count * band_local
    field_count = atom_count * chain_count
    total_count = (
        core_count * band_local * lax.axis_size("band") * kpoint_local * lax.axis_size("grid")
    )
    cas_grid = cas_table(grid_size)
    shifted = shift_axis(potential, sites[0, 0], 0)
    shifted = shift_axis(shifted, sites[1, 0], 1)
    shifted = shift_axis(shifted, sites[2, 0], 2)
    tables = [shifted]
    shifted_all = jnp.stack(tables, axis=-1)
    slab_table = lax.dynamic_slice_in_dim(shifted_all, position * plane_count, plane_count, 1)

    def moment(left, right):
        return jnp.sum(left * right, axis=(1, 3, 4)) / total_count

    start_sum = lax.psum(moment(start, start), ("grid", "band"))
    lanczos = start / expand_coef(jnp.sqrt(start_sum))
    previous = jnp.zeros_like(start)
    beta_prev = jnp.zeros((atom_count, pol_count), jnp.float32)
    alpha_list = []
    beta_list = []
    for iteration in range(ITERS):
        spread_fields = lanczos.reshape(atom_count, chain_count, plane_count, grid_size, grid_size)
        spread_over_z = jnp.einsum(
            "arpyz,wz->pywar", spread_fields, cas_grid, precision=precise_mode
        )
        spread_over_y = jnp.einsum(
            "pywar,uy->puwar", spread_over_z, cas_grid, precision=precise_mode
        )
        direct_spectrum = lax.all_to_all(
            spread_over_y.reshape(plane_count, grid_size, grid_size, field_count),
            "grid",
            split_axis=1,
            concat_axis=0,
            tiled=True,
        )
        field_shape = direct_spectrum.shape
        over_x = jnp.einsum("xvwf,tx->tvwf", direct_spectrum, cas_grid, precision=precise_mode)
        split_view = over_x.reshape(
            field_shape[0], field_shape[1], field_shape[2], atom_count, chain_count
        )
        scaled = split_view * slab_table[..., None]
        back_x = jnp.einsum("tvwar,xt->xvwar", scaled, cas_grid, precision=precise_mode)
        weighted = back_x.reshape(field_shape)
        direct_returned = lax.all_to_all(weighted, "grid", split_axis=0, concat_axis=1, tiled=True)
        fields = direct_returned.reshape(plane_count, grid_size, grid_size, atom_count, chain_count)
        over_z = jnp.einsum("pvwar,zw->pvzar", fields, cas_grid, precision=precise_mode)
        over_y = jnp.einsum("pvzar,yv->arpyz", over_z, cas_grid, precision=precise_mode)
        applied = energies[None, :, None] * lanczos - over_y.reshape(start.shape) / volume
        moments_all = lax.psum(
            (
                moment(lanczos, applied),
                moment(applied, applied),
                moment(lanczos, lanczos),
                moment(previous, previous),
                moment(previous, applied),
                moment(lanczos, previous),
            ),
            ("grid", "band"),
        )
        alpha_now = moments_all[0]
        square = (
            moments_all[1]
            + alpha_now * alpha_now * moments_all[2]
            + beta_prev * beta_prev * moments_all[3]
        )
        square = square - 2.0 * alpha_now * moments_all[0] - 2.0 * beta_prev * moments_all[4]
        square = square + 2.0 * alpha_now * beta_prev * moments_all[5]
        beta_now = jnp.sqrt(square)
        remainder = applied - expand_coef(alpha_now) * lanczos - expand_coef(beta_prev) * previous
        previous = lanczos
        lanczos = remainder / expand_coef(beta_now)
        beta_prev = beta_now
        alpha_list.append(alpha_now)
        beta_list.append(beta_now)
    return (jnp.stack(alpha_list, axis=2), jnp.stack(beta_list, axis=2), lanczos)


def solution(mesh):
    in_specs = (P(None, None, None, "band", "grid"), P(None, "band", "grid"), P(), P())
    out_specs = (P(), P(), P(None, None, None, "band", "grid"))
    return jax.shard_map(body, mesh=mesh, in_specs=in_specs, out_specs=out_specs, check_vma=False)
```

profile of v0, /device:TPU:0, one launch (start us, length us, event | category | flops | bytes accessed | tf_op | source)
XLA Modules:
  0.0 697.9 jit_solution(12863842465715470932)
XLA Ops:
  3.4 42.7 %psum.163 = f32[1,1]{1,0:T(1,128)} all-reduce(f32[1,1]{1,0:T(1,128)} %bitcast.1), channel_id=1, replica_groups=mesh['grid'=8,'band'=4] {'grid','band'}, use_global_device_ids=true, to_apply=%region_1.2 | all-reduce | flops 1 | bytes 8 | tf_op jit(solution)/shard_map/psum | solution.py:54
  48.0 2.7 reshape.300
  50.7 14.6 %fusion.60 = f32[4,32,32,64]{3,2,1,0:T(8,128)S(1)} fusion(f32[64,4,32,32]{3,2,1,0:T(8,128)} %reshape.300), kind=kOutput, calls=%fused_computation.48 | convolution fusion | flops 100678656 | bytes 2097152 | tf_op jit(solution)/shard_map/arpyz,wz->pywar/dot_general | solution.py:62
  65.4 3.0 fusion.40
  71.8 4.0 all-to-all-start
  79.0 12.1 %all-to-all-done = f32[8,1,32768]{2,1,0:T(1,128)S(1)} async-done(((f32[8,1,32768]{2,1,0:T(1,128)}), f32[8,1,32768]{2,1,0:T(1,128)S(1)}, u32[]{:S(2)}, u32[]{:S(2)}) %all-to-all-start) | async-done | bytes 1048608 | tf_op jit(solution)/shard_map/all_to_all | solution.py:68
  91.6 3.1 reduce.21
  95.8 3.0 fusion.28
  103.6 18.2 %all_to_all.132 = f32[8,1,32768]{2,1,0:T(1,128)S(1)} all-to-all(f32[8,1,32768]{2,1,0:T(1,128)S(1)} %reshape.323), channel_id=1, replica_groups=mesh['grid'=8,'band'=4] {'grid'}, dimensions={0} | all-to-all | bytes 2097152 | tf_op jit(solution)/shard_map/all_to_all | solution.py:83
  121.7 3.1 reduce.22
  127.9 3.0 multiply_bitcast_fusion.3
  130.9 4.5 copy.97
  135.5 3.7 div.203
  144.4 43.1 %all-reduce.3 = (f32[1,1]{1,0:T(1,128)}, f32[1,1]{1,0:T(1,128)}, f32[1,1]{1,0:T(1,128)}, f32[1,1]{1,0:T(1,128)}, f32[1,1]{1,0:T(1,128)}, /*index=5*/f32[1,1]{1,0:T(1,128)}) all-reduce(f32[1,1]{1,0:T(1,128)} %bitcast.31, f32[1,1]{1,0:T(1,128)} %bitcast.28, f32[1,1]{1,0:T(1,128)} %bitcast.32, ...), channel_id=1, replica_groups=mesh['grid'=8,'band'=4] {'grid','band'}, use_global_device_ids=true, to_apply=%region_5.6 | all-reduce | flops 6 | bytes 48 | tf_op jit(solution)/shard_map/psum | solution.py:88
  195.4 2.7 reshape.305
  198.1 14.6 %fusion.63 = f32[4,32,32,64]{3,2,1,0:T(8,128)S(1)} fusion(f32[64,4,32,32]{3,2,1,0:T(8,128)} %reshape.305), kind=kOutput, calls=%fused_computation.49 | convolution fusion | flops 100678656 | bytes 2097152 | tf_op jit(solution)/shard_map/arpyz,wz->pywar/dot_general | solution.py:62
  212.7 3.0 fusion.45
  218.3 3.3 reshape.325
  221.6 19.8 %all_to_all.133 = f32[8,1,32768]{2,1,0:T(1,128)} all-to-all(f32[8,1,32768]{2,1,0:T(1,128)} %reshape.325), channel_id=1, replica_groups=mesh['grid'=8,'band'=4] {'grid'}, dimensions={0} | all-to-all | bytes 2097152 | tf_op jit(solution)/shard_map/all_to_all | solution.py:68
  241.4 5.3 reduce.23
  246.7 3.4 reshape.326
  252.0 3.0 fusion.22
  259.7 3.3 reshape.327
  263.0 4.6 all-to-all-start.3
  268.3 14.8 %all-to-all-done.3 = f32[8,1,32768]{2,1,0:T(1,128)} async-done(((f32[8,1,32768]{2,1,0:T(1,128)}), f32[8,1,32768]{2,1,0:T(1,128)}, u32[]{:S(2)}, u32[]{:S(2)}) %all-to-all-start.3) | async-done | bytes 1048608 | tf_op jit(solution)/shard_map/all_to_all | solution.py:83
  283.1 5.3 reduce.24
  288.4 3.4 reshape.328
  295.6 4.4 multiply_bitcast_fusion.2
  299.9 5.6 copy.107
  305.5 4.3 div.220
  309.8 3.3 multiply_reduce_fusion.10
  316.3 41.5 %all-reduce.2 = (f32[1,1]{1,0:T(1,128)}, f32[1,1]{1,0:T(1,128)}, f32[1,1]{1,0:T(1,128)}, f32[1,1]{1,0:T(1,128)}, f32[1,1]{1,0:T(1,128)}) all-reduce(f32[1,1]{1,0:T(1,128)} %bitcast.57, f32[1,1]{1,0:T(1,128)} %bitcast.54, f32[1,1]{1,0:T(1,128)} %bitcast.58, f32[1,1]{1,0:T(1,128)} %bitcast.59, ...), channel_id=1, replica_groups=mesh['grid'=8,'band'=4] {'grid','band'}, use_global_device_ids=true, to_apply=%region_16.17 | all-reduce | flops 5 | bytes 40 | tf_op jit(solution)/shard_map/psum | solution.py:88
  364.9 2.7 reshape.310
  367.6 14.6 %fusion.66 = f32[4,32,32,64]{3,2,1,0:T(8,128)S(1)} fusion(f32[64,4,32,32]{3,2,1,0:T(8,128)} %reshape.310), kind=kOutput, calls=%fused_computation.50 | convolution fusion | flops 100678656 | bytes 2097152 | tf_op jit(solution)/shard_map/arpyz,wz->pywar/dot_general | solution.py:62
  382.2 3.0 fusion.50
  390.4 19.2 %all_to_all.134 = f32[8,1,32768]{2,1,0:T(1,128)} all-to-all(f32[8,1,32768]{2,1,0:T(1,128)S(1)} %reshape.329), channel_id=1, replica_groups=mesh['grid'=8,'band'=4] {'grid'}, dimensions={0} | all-to-all | bytes 2097152 | tf_op jit(solution)/shard_map/all_to_all | solution.py:68
  409.6 4.4 reduce.25
  418.0 3.0 fusion.16
  425.7 3.3 reshape.331
  429.0 4.6 all-to-all-start.5
  434.3 14.8 %all-to-all-done.5 = f32[8,1,32768]{2,1,0:T(1,128)} async-done(((f32[8,1,32768]{2,1,0:T(1,128)}), f32[8,1,32768]{2,1,0:T(1,128)}, u32[]{:S(2)}, u32[]{:S(2)}) %all-to-all-start.5) | async-done | bytes 1048608 | tf_op jit(solution)/shard_map/all_to_all | solution.py:83
  449.1 4.4 reduce.26
  459.4 4.4 multiply_bitcast_fusion.1
  463.7 5.6 copy.117
  469.3 4.4 div.237
  473.7 3.3 multiply_reduce_fusion.5
  480.2 42.5 %all-reduce.1 = (f32[1,1]{1,0:T(1,128)}, f32[1,1]{1,0:T(1,128)}, f32[1,1]{1,0:T(1,128)}, f32[1,1]{1,0:T(1,128)}, f32[1,1]{1,0:T(1,128)}) all-reduce(f32[1,1]{1,0:T(1,128)} %bitcast.83, f32[1,1]{1,0:T(1,128)} %bitcast.80, f32[1,1]{1,0:T(1,128)} %bitcast.84, f32[1,1]{1,0:T(1,128)} %bitcast.85, ...), channel_id=1, replica_groups=mesh['grid'=8,'band'=4] {'grid','band'}, use_global_device_ids=true, to_apply=%region_26.27 | all-reduce | flops 5 | bytes 40 | tf_op jit(solution)/shard_map/psum | solution.py:88
  529.5 2.7 reshape.315
  532.2 14.6 %fusion.69 = f32[4,32,32,64]{3,2,1,0:T(8,128)S(1)} fusion(f32[64,4,32,32]{3,2,1,0:T(8,128)} %reshape.315), kind=kOutput, calls=%fused_computation.51 | convolution fusion | flops 100678656 | bytes 2097152 | tf_op jit(solution)/shard_map/arpyz,wz->pywar/dot_general | solution.py:62
  546.8 3.0 fusion.55
  555.0 19.3 %all_to_all.135 = f32[8,1,32768]{2,1,0:T(1,128)} all-to-all(f32[8,1,32768]{2,1,0:T(1,128)S(1)} %reshape.333), channel_id=1, replica_groups=mesh['grid'=8,'band'=4] {'grid'}, dimensions={0} | all-to-all | bytes 2097152 | tf_op jit(solution)/shard_map/all_to_all | solution.py:68
  574.3 4.4 reduce.27
  582.6 3.0 fusion.10
  590.4 3.3 reshape.335
  593.7 4.5 all-to-all-start.7
  598.8 14.8 %all-to-all-done.7 = f32[8,1,32768]{2,1,0:T(1,128)} async-done(((f32[8,1,32768]{2,1,0:T(1,128)}), f32[8,1,32768]{2,1,0:T(1,128)}, u32[]{:S(2)}, u32[]{:S(2)}) %all-to-all-start.7) | async-done | bytes 1048608 | tf_op jit(solution)/shard_map/all_to_all | solution.py:83
  613.6 4.4 reduce.28
  623.9 4.4 multiply_bitcast_fusion
  628.2 5.6 copy.127
  633.8 4.4 div.254
  638.2 3.3 multiply_reduce_fusion
  644.8 41.3 %all-reduce = (f32[1,1]{1,0:T(1,128)}, f32[1,1]{1,0:T(1,128)}, f32[1,1]{1,0:T(1,128)}, f32[1,1]{1,0:T(1,128)}, f32[1,1]{1,0:T(1,128)}) all-reduce(f32[1,1]{1,0:T(1,128)} %bitcast.106, f32[1,1]{1,0:T(1,128)} %bitcast.111, f32[1,1]{1,0:T(1,128)} %bitcast.112, ...), channel_id=1, replica_groups=mesh['grid'=8,'band'=4] {'grid','band'}, use_global_device_ids=true, to_apply=%region_34.35 | all-reduce | flops 5 | bytes 40 | tf_op jit(solution)/shard_map/psum | solution.py:88
  691.4 3.1 divide_bitcast_fusion
  694.5 3.0 pad_maximum_fusion
  (58 shorter events, 77.6 us)
Async XLA Ops:
  69.6 6.2 copy-start.5
  69.6 8.8 %copy-start.4 = (f32[32,32,32]{2,1,0:T(8,128)S(1)}, f32[32,32,32]{2,1,0:T(8,128)}, u32[]{:S(2)}) copy-start(f32[32,32,32]{2,1,0:T(8,128)} %param.7) | copy-start | bytes 393220
  71.8 19.3 %all-to-all-start = ((f32[8,1,32768]{2,1,0:T(1,128)}), f32[8,1,32768]{2,1,0:T(1,128)S(1)}, u32[]{:S(2)}, u32[]{:S(2)}) async-start(f32[8,1,32768]{2,1,0:T(1,128)} %reshape.321), calls=%async_computation | async-start | bytes 2097152 | tf_op jit(solution)/shard_map/all_to_all | solution.py:68
  135.5 3.7 copy-start
  135.5 3.7 copy-start.1
  263.0 20.0 %all-to-all-start.3 = ((f32[8,1,32768]{2,1,0:T(1,128)}), f32[8,1,32768]{2,1,0:T(1,128)}, u32[]{:S(2)}, u32[]{:S(2)}) async-start(f32[8,1,32768]{2,1,0:T(1,128)} %reshape.327), calls=%async_computation.3 | async-start | bytes 2097152 | tf_op jit(solution)/shard_map/all_to_all | solution.py:83
  429.0 20.0 %all-to-all-start.5 = ((f32[8,1,32768]{2,1,0:T(1,128)}), f32[8,1,32768]{2,1,0:T(1,128)}, u32[]{:S(2)}, u32[]{:S(2)}) async-start(f32[8,1,32768]{2,1,0:T(1,128)} %reshape.331), calls=%async_computation.5 | async-start | bytes 2097152 | tf_op jit(solution)/shard_map/all_to_all | solution.py:83
  469.3 4.4 copy-start.2
  593.7 19.9 %all-to-all-start.7 = ((f32[8,1,32768]{2,1,0:T(1,128)}), f32[8,1,32768]{2,1,0:T(1,128)}, u32[]{:S(2)}, u32[]{:S(2)}) async-start(f32[8,1,32768]{2,1,0:T(1,128)} %reshape.335), calls=%async_computation.7 | async-start | bytes 2097152 | tf_op jit(solution)/shard_map/all_to_all | solution.py:83
  633.8 4.4 copy-start.3
where the time goes:
time: 709 us; the launch traced here: 698 us
  blocking collectives  287 us (40%)
  local copies, waits for them, and re-layouts  118 us (17%)
  matrix products  115 us (16%)
  other arithmetic  62.4 us (9%)
  waiting for transfers between devices  56.4 us (8%)
  between operations  40.5 us (6%)
  starting transfers between devices  17.7 us (2%)
    psum x4, blocking collectives, body(): lax.psum((moment(lanczos, applied), moment(applied, applied), moment(lanc...  168 us
    dot_general x4, matrix products, body(): jnp.einsum('arpyz,wz->pywar', spread_fields, cas_grid, precision=precise_...  58.4 us
    all_to_all x3, blocking collectives, body(): lax.all_to_all(spread_over_y.reshape(plane_count, grid_size, grid_size, f...  58.3 us
    all_to_all x3, waiting for transfers between devices, body(): lax.all_to_all(weighted, 'grid', split_axis=0, concat_axis=1, tiled=True)  44.3 us
    psum x1, blocking collectives, body(): start_sum = lax.psum(moment(start, start), ('grid', 'band'))  42.7 us
    unnamed x28, local copies, waits for them, and re-layouts  39.2 us
    div x8, local copies, waits for them, and re-layouts, body(): over_y.reshape(start.shape) / volume  38.1 us
    all_to_all x1, blocking collectives, body(): lax.all_to_all(weighted, 'grid', split_axis=0, concat_axis=1, tiled=True)  18.2 us
  transfers between devices with their start and end apart: 4, of which 4 were waited for; matrix products, arithmetic and copies ran while one was open for 0% of the time, Pallas kernels for 0%

commit v1 on v0

v1 whole, which is shorter than its diff:
```python
import functools
import math

import jax
import jax.numpy as jnp
import numpy as np
from jax import lax
from jax.experimental import pallas as pl
from jax.experimental.pallas import tpu as pltpu
from jax.sharding import PartitionSpec as P

ITERS = 4
LANES = 128
RADIX = 8
PAIRS = 4
RESIDUES = ((0, 4), (1, 7), (2, 6), (3, 5))
HALF_ROOT = math.sqrt(0.5)
ROW_BETA = 8
ROW_NORM = 16
ROW_LAST = 17
ROWS = 24


def cas(angle):
    return np.cos(angle) + np.sin(angle)


@functools.cache
def pair_weights(size):
    low = size // RADIX
    cells = np.arange(size)
    over_z = cas(2 * np.pi * np.outer(cells, cells) / size)
    weights = np.zeros((PAIRS, 2, low, size, 2, low, size))
    for pair, residues in enumerate(RESIDUES):
        for out_half, residue in enumerate(residues):
            for v0 in range(low):
                for y0 in range(low):
                    angle = 2 * np.pi * (residue + RADIX * v0) * y0 / size
                    cosine, sine = np.cos(angle), np.sin(angle)
                    if pair == 0:
                        weights[pair, out_half, y0, :, out_half, v0] = (cosine + sine) * over_z
                    else:
                        sign = 1.0 if out_half == 0 else -1.0
                        weights[pair, 0, y0, :, out_half, v0] = (cosine + sine) * over_z
                        weights[pair, 1, y0, :, out_half, v0] = sign * (cosine - sine) * over_z
    return weights.reshape(PAIRS, 2 * low * size, 2 * low * size)


def split_weights(weights):
    high = weights.astype(np.float32).astype(jnp.bfloat16)
    rest = (weights - high.astype(np.float64)).astype(np.float32).astype(jnp.bfloat16)
    return high, rest


def hartley(values):
    count = len(values)
    if count == 2:
        return [values[0] + values[1], values[0] - values[1]]
    even, odd = hartley(values[0::2]), hartley(values[1::2])
    half = count // 2
    first, second = [], []
    for u in range(half):
        angle = 2 * math.pi * u / count
        if u == 0:
            turned = odd[0]
        elif 4 * u == count:
            turned = odd[u]
        elif 8 * u == count:
            turned = (odd[u] + odd[half - u]) * HALF_ROOT
        elif 8 * u == 3 * count:
            turned = (odd[half - u] - odd[u]) * HALF_ROOT
        else:
            turned = odd[u] * math.cos(angle) + odd[half - u] * math.sin(angle)
        first.append(even[u] + turned)
        second.append(even[u] - turned)
    return first + second


def butterflies(f):
    a = [f[i] + f[i + 4] for i in range(4)]
    b = [f[i] - f[i + 4] for i in range(4)]
    even, odd = a[0] + a[2], a[1] + a[3]
    less, more = (b[1] - b[3]) * HALF_ROOT, (b[1] + b[3]) * HALF_ROOT
    return (
        (even + odd, even - odd),
        (b[0] + less, b[2] + more),
        (a[0] - a[2], a[1] - a[3]),
        (b[0] - less, more - b[2]),
    )


def butterflies_back(pairs):
    (c0, c4), (c1, s1), (c2, s2), (c3, s3) = pairs
    even, odd = c0 + c4, c0 - c4
    less, more = (c1 - c3) * HALF_ROOT, (s1 + s3) * HALF_ROOT
    a = [even + c2, odd + s2, even - c2, odd - s2]
    b = [c1 + c3, less + more, s1 - s3, more - less]
    return [a[i] + b[i] for i in range(4)] + [a[i] - b[i] for i in range(4)]


def total(block):
    return jnp.sum(jnp.sum(block, axis=0, keepdims=True), axis=1, keepdims=True)


def guarded(square):
    root = jnp.sqrt(square)
    positive = root > 0.0
    return root, jnp.where(positive, 1.0 / jnp.where(positive, root, 1.0), 0.0)


def matmul3(value, high_ref, rest_ref, pair):
    high = value.astype(jnp.bfloat16)
    rest = (value - high.astype(jnp.float32)).astype(jnp.bfloat16)
    dot = functools.partial(jnp.dot, preferred_element_type=jnp.float32)
    return dot(high, high_ref[pair]) + (dot(rest, high_ref[pair]) + dot(high, rest_ref[pair]))


def recur_kernel(
    size, both_ref, pot_ref, fwd_high, fwd_rest, back_high, back_rest,
    basis_ref, message_ref, own_ref, left, right,
):
    groups, double, width = both_ref.shape
    fields = double // 2
    planes = width // (size * size)

    def rows_of(group, plane):
        return pl.ds(pl.multiple_of((group * planes + plane) * fields, 8), fields)

    def cut(plane, block):
        start = (plane * RADIX + block) * LANES
        return slice(start, start + LANES)

    def over_planes(step, init):
        def run(group, carry):
            for plane in range(planes):
                carry = step(group, plane, carry)
            return carry

        return lax.fori_loop(0, groups, run, init)

    zero = jnp.zeros((fields, LANES), jnp.float32)

    def take_start(group, plane, carry):
        for block in range(RADIX):
            value = both_ref[group, :fields, cut(plane, block)]
            basis_ref[0, group, :, cut(plane, block)] = value
            carry = carry + value * value
        return carry

    norm, scale = guarded(total(over_planes(take_start, zero)))
    row = lax.broadcasted_iota(jnp.int32, (ROWS, LANES), 0)
    stats = jnp.where(row == ROW_NORM, norm, 0.0)

    def iteration(step, state):
        stats, scale, beta_prev = state
        before = jnp.maximum(step - 1, 0)

        def forward(group, plane, carry):
            values = []
            for block in range(RADIX):
                value = basis_ref[step, group, :, cut(plane, block)] * scale
                basis_ref[step, group, :, cut(plane, block)] = value
                values.append(value)
            for pair, halves in enumerate(butterflies(values)):
                for half, value in enumerate(halves):
                    left[pair, rows_of(group, plane), half * LANES : (half + 1) * LANES] = value
            return carry

        over_planes(forward, 0)

        def middle(pair, carry):
            right[pair] = matmul3(left[pair], fwd_high, fwd_rest, pair)
            for half in range(2):
                lanes = slice(half * LANES, (half + 1) * LANES)
                column = [right[pair, x * fields : (x + 1) * fields, lanes] for x in range(size)]
                column = hartley(column)
                column = [column[x] * pot_ref[pair, x : x + 1, lanes] for x in range(size)]
                column = hartley(column)
                for x in range(size):
                    left[pair, x * fields : (x + 1) * fields, lanes] = column[x]
            right[pair] = matmul3(left[pair], back_high, back_rest, pair)
            return carry

        lax.fori_loop(0, PAIRS, middle, 0)

        def backward(group, plane, carry):
            pairs = []
            for pair in range(PAIRS):
                pairs.append(
                    [
                        right[pair, rows_of(group, plane), half * LANES : (half + 1) * LANES]
                        for half in range(2)
                    ]
                )
            for block, direct in enumerate(butterflies_back(pairs)):
                place = cut(plane, block)
                value = basis_ref[step, group, :, place]
                applied = both_ref[group, fields:, place] * value - direct
                applied = applied - beta_prev * basis_ref[before, group, :, place]
                basis_ref[step + 1, group, :, place] = applied
                carry = carry + value * applied
            return carry

        alpha = total(over_planes(backward, zero))

        def remove(group, plane, carry):
            for block in range(RADIX):
                place = cut(plane, block)
                value = basis_ref[step + 1, group, :, place]
                value = value - alpha * basis_ref[step, group, :, place]
                basis_ref[step + 1, group, :, place] = value
                carry = carry + value * value
            return carry

        beta, scale = guarded(total(over_planes(remove, zero)))
        stats = jnp.where(row == step, alpha, stats)
        stats = jnp.where(row == step + ROW_BETA, beta, stats)
        return jnp.where(row == ROW_LAST, scale, stats), scale, beta

    one = jnp.zeros((1, 1), jnp.float32)
    stats, _, _ = lax.fori_loop(0, ITERS, iteration, (stats, scale, one))
    own_ref[...] = stats
    lane = lax.broadcasted_iota(jnp.int32, (1, LANES), 1)
    message = jnp.zeros((1, LANES), jnp.float32)
    for place in [*range(ITERS), *range(ROW_BETA, ROW_BETA + ITERS), ROW_NORM]:
        message = jnp.where(lane == place, stats[place : place + 1], message)
    message_ref[...] = jnp.broadcast_to(message[None], message_ref.shape)


def combine_kernel(
    root_count, planes, all_ref, own_ref, basis_ref, result_ref, alpha_ref, beta_ref
):
    groups, fields, width = result_ref.shape
    table = jnp.transpose(all_ref[:, 0, :])
    wide_alpha, wide_beta = table[0:8], table[8:16]
    own_alpha, own_beta = own_ref[0:8], own_ref[8:16]
    square = table[ROW_NORM : ROW_NORM + 1]
    _, inverse = guarded(total(square * square))

    def first(norm, like):
        row = lax.broadcasted_iota(jnp.int32, like.shape, 0)
        return jnp.where(row == 0, norm * inverse, 0.0)

    def apply(diagonal, side, vector):
        return diagonal * vector + side * pltpu.roll(vector, 7, 0) + pltpu.roll(side * vector, 1, 0)

    wide = first(square, wide_alpha)
    own = first(own_ref[ROW_NORM : ROW_NORM + 1], own_alpha)
    wide_prev, own_prev = jnp.zeros_like(wide), jnp.zeros_like(own)
    beta = jnp.zeros((1, 1), jnp.float32)
    lane = lax.broadcasted_iota(jnp.int32, (1, LANES), 1)
    alphas = jnp.zeros((1, LANES), jnp.float32)
    betas = jnp.zeros((1, LANES), jnp.float32)
    for step in range(ITERS):
        applied = apply(wide_alpha, wide_beta, wide)
        alpha = total(wide * applied)
        remainder = applied - alpha * wide - beta * wide_prev
        own_remainder = apply(own_alpha, own_beta, own) - alpha * own - beta * own_prev
        beta = jnp.sqrt(total(remainder * remainder))
        wide_prev, own_prev = wide, own
        wide, own = remainder / beta, own_remainder / beta
        alphas = jnp.where(lane == step, alpha, alphas)
        betas = jnp.where(lane == step, beta, betas)
    alpha_ref[0] = alphas[:, :ITERS]
    beta_ref[0] = betas[:, :ITERS]
    factors = [own[i : i + 1] * root_count for i in range(ITERS + 1)]
    factors[ITERS] = factors[ITERS] * own_ref[ROW_LAST : ROW_LAST + 1]

    def run(group, carry):
        for block in range(width // LANES):
            place = slice(block * LANES, (block + 1) * LANES)
            value = basis_ref[0, group, :, place] * factors[0]
            for i in range(1, ITERS + 1):
                value = value + basis_ref[i, group, :, place] * factors[i]
            result_ref[group, :, place] = value
        return carry

    lax.fori_loop(0, groups, run, 0)


def shift_axis(part, offset, axis_number):
    length = part.shape[axis_number]
    doubled = jnp.concatenate([part, part], axis=axis_number)
    first_index = (length - offset) % length
    return lax.dynamic_slice_in_dim(doubled, first_index, length, axis_number)


def potential_table(potential, sites):
    size = potential.shape[0]
    table = potential
    for axis in range(3):
        table = shift_axis(table, sites[axis, 0], axis)
    table = table * (1.0 / size**3)
    table = table.reshape(size, size // RADIX, RADIX, size)
    pairs = [
        jnp.concatenate([table[:, :, residue].reshape(size, -1) for residue in residues], axis=1)
        for residues in RESIDUES
    ]
    return jnp.stack(pairs)


def body(start, energies, sites, potential):
    size = potential.shape[0]
    atom_count, core_count, pol_count, band_local, kpoint_local = start.shape
    assert atom_count == 1 and pol_count == 1 and size * (size // RADIX) == LANES
    groups = lax.axis_size("grid")
    devices = groups * lax.axis_size("band")
    chain = core_count * band_local
    planes = size // groups
    fields = -(-chain // groups)
    padded = -(-fields // 8) * 8

    def by_owner(part):
        part = part.reshape(chain, kpoint_local)
        if fields * groups != chain:
            part = jnp.pad(part, ((0, fields * groups - chain), (0, 0)))
        part = part.reshape(groups, fields, kpoint_local)
        if padded != fields:
            part = jnp.pad(part, ((0, 0), (0, padded - fields), (0, 0)))
        return part

    both = jnp.concatenate([by_owner(start), by_owner(energies)], axis=1)
    both = lax.all_to_all(both, "grid", split_axis=0, concat_axis=0, tiled=True)
    table = potential_table(potential, sites)
    weights = pair_weights(size)
    fwd_high, fwd_rest = split_weights(weights)
    back_high, back_rest = split_weights(weights.transpose(0, 2, 1))
    vmem = pl.BlockSpec(memory_space=pltpu.VMEM)
    shape = functools.partial(jax.ShapeDtypeStruct, dtype=jnp.float32)
    pair_shape = (PAIRS, size * padded, 2 * LANES)
    basis, message, own = pl.pallas_call(
        functools.partial(recur_kernel, size),
        out_shape=(
            shape((ITERS + 1, groups, padded, kpoint_local)),
            shape((devices, 1, LANES)),
            shape((ROWS, LANES)),
        ),
        in_specs=[vmem] * 6,
        out_specs=(vmem, vmem, vmem),
        scratch_shapes=[pltpu.VMEM(pair_shape, jnp.float32)] * 2,
        compiler_params=pltpu.CompilerParams(vmem_limit_bytes=24 * 2**20),
        name="recur",
    )(both, table, *map(jnp.asarray, (fwd_high, fwd_rest, back_high, back_rest)))
    gathered = lax.all_to_all(message, ("grid", "band"), split_axis=0, concat_axis=0, tiled=True)
    count = chain * lax.axis_size("band") * kpoint_local * groups
    result, alphas, betas = pl.pallas_call(
        functools.partial(combine_kernel, math.sqrt(count), planes),
        out_shape=(
            shape((groups, padded, kpoint_local)),
            shape((1, 1, ITERS)),
            shape((1, 1, ITERS)),
        ),
        in_specs=[vmem] * 3,
        out_specs=(vmem, vmem, vmem),
        compiler_params=pltpu.CompilerParams(vmem_limit_bytes=16 * 2**20),
        name="combine",
    )(gathered, own, basis)
    back = lax.all_to_all(result, "grid", split_axis=0, concat_axis=0, tiled=True)
    back = back[:, :fields].reshape(groups * fields, kpoint_local)[:chain]
    return alphas, betas, back.reshape(start.shape)


def solution(mesh):
    in_specs = (P(None, None, None, "band", "grid"), P(None, "band", "grid"), P(), P())
    out_specs = (P(), P(), P(None, None, None, "band", "grid"))
    return jax.shard_map(body, mesh=mesh, in_specs=in_specs, out_specs=out_specs, check_vma=False)
```

time: 709 us -> 90.5 us (0.13); the launches traced: 698 us -> 89.9 us
  blocking collectives: 287 us -> 28.8 us
  matrix products: 115 us -> 0 us
  local copies, waits for them, and re-layouts: 118 us -> 8.28 us
  other arithmetic: 62.4 us -> 5.23 us
  waiting for transfers between devices: 56.4 us -> 17.2 us
  between operations: 40.5 us -> 2.71 us
  Pallas kernels: 0 us -> 22.4 us
  starting transfers between devices: 17.7 us -> 5.33 us
    psum x5 -> x0, blocking collectives: 211 us -> none  [the longest x4 168 us: body(): lax.psum((moment(lanczos, applied), moment(applied, applied), moment(lanc...]
    dot_general x24 -> x0, matrix products: 115 us -> none  [the longest x4 58.4 us: body(): jnp.einsum('arpyz,wz->pywar', spread_fields, cas_grid, precision=precise_...]
    all_to_all x4 -> x2, blocking collectives: 76.5 us -> 28.8 us  [the longest x1 17.7 us: body(): lax.all_to_all(result, 'grid', split_axis=0, concat_axis=0, tiled=True)]
    all_to_all x4 -> x1, waiting for transfers between devices: 56.4 us -> 17.2 us  [body(): both = lax.all_to_all(both, 'grid', split_axis=0, concat_axis=0, tiled=True)]
    div x8 -> x0, local copies, waits for them, and re-layouts: 38.1 us -> none  [body(): over_y.reshape(start.shape) / volume]
    unnamed x28 -> x13, local copies, waits for them, and re-layouts: 39.2 us -> 3.07 us
    all_to_all x8 -> x0, other arithmetic: 34.4 us -> none  [the longest x4 17.2 us: body(): lax.all_to_all(weighted, 'grid', split_axis=0, concat_axis=1, tiled=True)]
    pallas_call x0 -> x2, Pallas kernels: none -> 22.4 us  [the longest x1 20.7 us: body(): pl.pallas_call(functools.partial(recur_kernel, size), out_shape=(shape((I...]
  transfers between devices with their start and end apart: 4 -> 1, of which waited for: 4 -> 1; matrix products, arithmetic and copies ran while one was open for 0% -> 8% of each run, Pallas kernels for 0% -> 0%
where the time goes in v1:
time: 90.5 us; the launch traced here: 89.9 us
  blocking collectives  28.8 us (32%)
  Pallas kernels  22.4 us (25%)
  waiting for transfers between devices  17.2 us (19%)
  local copies, waits for them, and re-layouts  8.28 us (9%)
  starting transfers between devices  5.33 us (6%)
  other arithmetic  5.23 us (6%)
  between operations  2.71 us (3%)
    pallas_call x1, Pallas kernels, body(): pl.pallas_call(functools.partial(recur_kernel, size), out_shape=(shape((I...  20.7 us
    all_to_all x1, blocking collectives, body(): lax.all_to_all(result, 'grid', split_axis=0, concat_axis=0, tiled=True)  17.7 us
    all_to_all x1, waiting for transfers between devices, body(): both = lax.all_to_all(both, 'grid', split_axis=0, concat_axis=0, tiled=True)  17.2 us
    all_to_all x1, blocking collectives, body(): lax.all_to_all(message, ('grid', 'band'), split_axis=0, concat_axis=0, ti...  11 us
    all_to_all x1, starting transfers between devices, body(): both = lax.all_to_all(both, 'grid', split_axis=0, concat_axis=0, tiled=True)  5.33 us
    another operation x8, local copies, waits for them, and re-layouts, potential_table(): table[:, :, residue].reshape(size, -1)  3.63 us
    unnamed x13, local copies, waits for them, and re-layouts  3.07 us
    concatenate x1, other arithmetic, body(): both = jnp.concatenate([by_owner(start), by_owner(energies)], axis=1)  3.07 us
  transfers between devices with their start and end apart: 1, of which 1 were waited for; matrix products, arithmetic and copies ran while one was open for 8% of the time, Pallas kernels for 0%

profile of v1, /device:TPU:0, one launch (start us, length us, event | category | flops | bytes accessed | tf_op | source)
XLA Modules:
  0.0 89.9 jit_solution(7054181123740881812)
XLA Ops:
  0.6 3.1 %pad_maximum_fusion = f32[8,16,4096]{2,1,0:T(8,128)} fusion(f32[8,8,4096]{2,1,0:T(8,128)} %bitcast.43, f32[8,8,4096]{2,1,0:T(8,128)} %bitcast.44), kind=kLoop, calls=%fused_computation | loop fusion | flops 524288 | bytes 4194304 | tf_op jit(solution)/shard_map/concatenate | solution.py:322
  3.7 0.0 copy-start.5
  3.7 0.0 copy-start.4
  3.7 5.3 %all-to-all-start = ((f32[8,16,4096]{2,1,0:T(8,128)}), f32[8,16,4096]{2,1,0:T(8,128)S(1)}, u32[]{:S(2)}, u32[]{:S(2)}) async-start(f32[8,16,4096]{2,1,0:T(8,128)} %pad_maximum_fusion), calls=%async_computation | async-start | bytes 4194304 | tf_op jit(solution)/shard_map/all_to_all | solution.py:323
  9.0 0.0 copy-done.5
  9.0 0.6 fusion.5
  11.6 0.0 copy-done.4
  11.6 0.2 fusion.1
  11.8 0.0 copy-start
  11.8 0.0 copy-start.1
  11.8 0.2 fusion
  12.0 0.3 fusion.3
  12.4 1.0 %fusion.4 = (f32[32,4,1,32]{3,2,1,0:T(1,128)}, f32[32,4,1,32]{3,2,1,0:T(1,128)}, f32[32,4,1,32]{3,2,1,0:T(1,128)S(1)}, f32[32,4,1,32]{3,2,1,0:T(1,128)S(1)}, f32...) fusion(f32[32,4,8,32]{3,2,1,0:T(8,128)S(1)} %fusion.3), kind=kLoop, calls=%fused_computation.15 | loop fusion | bytes 262144 | tf_op jit(solution)/shard_map/slice | solution.py:296
  13.4 1.5 %reshape_squeeze.24 = f32[32,128]{1,0:T(8,128)} reshape(f32[32,4,1,32]{3,1,0,2:T(4,128)} %bitcast.52) | data formatting | bytes 32768 | tf_op jit(solution)/shard_map/reshape;squeeze | solution.py:296
  14.9 0.9 %reshape_squeeze.30 = f32[32,128]{1,0:T(8,128)S(1)} reshape(f32[32,4,1,32]{3,1,0,2:T(4,128)} %bitcast.51) | data formatting | bytes 32768 | tf_op jit(solution)/shard_map/reshape;squeeze | solution.py:296
  15.8 0.7 reshape_squeeze.29
  16.5 0.1 reshape_squeeze.28
  16.6 0.1 reshape_squeeze.27
  16.7 0.1 reshape_squeeze.26
  16.8 0.1 reshape_squeeze.25
  16.9 0.1 reshape_squeeze.31
  17.0 0.7 maximum_bitcast_fusion
  17.7 0.7 maximum_bitcast_fusion.2
  18.5 17.2 %all-to-all-done.both_ref = f32[8,16,4096]{2,1,0:T(8,128)S(1)} async-done(((f32[8,16,4096]{2,1,0:T(8,128)}), f32[8,16,4096]{2,1,0:T(8,128)S(1)}, u32[]{:S(2)}, u32[]{:S(2)}) %all-to-all-start) | async-done | bytes 2097184 | tf_op jit(solution)/shard_map/all_to_all | solution.py:323
  35.6 0.0 copy-done
  35.7 0.0 copy-done.1
  35.7 0.0 copy-start.2
  35.7 1.0 %copy-done.2 = bf16[4,256,256]{2,1,0:T(8,128)(2,1)S(1)} copy-done((bf16[4,256,256]{2,1,0:T(8,128)(2,1)S(1)}, bf16[4,256,256]{2,1,0:T(8,128)(2,1)}, u32[]{:S(2)}) %copy-start.2) | copy-done | bytes 524312
  36.7 0.0 copy-start.3
  36.7 1.0 %copy-done.3 = bf16[4,256,256]{2,1,0:T(8,128)(2,1)S(1)} copy-done((bf16[4,256,256]{2,1,0:T(8,128)(2,1)S(1)}, bf16[4,256,256]{2,1,0:T(8,128)(2,1)}, u32[]{:S(2)}) %copy-start.3) | copy-done | bytes 524312
  37.7 20.7 %recur.1 = (f32[5,8,8,4096]{3,2,1,0:T(8,128)S(1)}, f32[32,1,128]{2,1,0:T(1,128)S(1)}, f32[24,128]{1,0:T(8,128)S(1)}) custom-call(f32[8,16,4096]{2,1,0:T(8,128)S(1)} %all-to-all-done.both_ref, f32[4,32,256]{2,1,0:T(8,128)S(1)} %pad_maximum_fusion.1.pot_ref, bf16[4,256,256]{2,1,0:T(8,128)(2,1)S(1)} %copy-done.3, bf16[4,256,256]{2,1,0:T(8,128)(2,1)S(1)} %copy-done.2, ...), custom_call_target="tpu_custom_call" | custom-call | tf_op jit(solution)/shard_map/recur/pallas_call | solution.py:331
  58.4 11.0 %all_to_all.15.all_ref = f32[32,1,128]{2,1,0:T(1,128)S(1)} all-to-all(f32[32,1,128]{2,1,0:T(1,128)S(1)} %get-tuple-element.9), channel_id=1, replica_groups=mesh['grid'=8,'band'=4] {'grid','band'}, dimensions={0} | all-to-all | bytes 32768 | tf_op jit(solution)/shard_map/all_to_all | solution.py:344
  69.4 1.8 %combine.1 = (f32[8,8,4096]{2,1,0:T(8,128)S(1)}, f32[1,1,4]{2,1,0:T(1,128)}, f32[1,1,4]{2,1,0:T(1,128)}) custom-call(f32[32,1,128]{2,1,0:T(1,128)S(1)} %all_to_all.15.all_ref, f32[24,128]{1,0:T(8,128)S(1)} %get-tuple-element.10.own_ref, f32[5,8,8,4096]{3,2,1,0:T(8,128)S(1)} %get-tuple-element.11.basis_ref), custom_call_target="tpu_custom_call" | custom-call | tf_op jit(solution)/shard_map/combine/pallas_call | solution.py:346
  71.2 17.7 %all_to_all.16 = f32[8,8,4096]{2,1,0:T(8,128)S(1)} all-to-all(f32[8,8,4096]{2,1,0:T(8,128)S(1)} %get-tuple-element.14), channel_id=1, replica_groups=mesh['grid'=8,'band'=4] {'grid'}, dimensions={0} | all-to-all | bytes 2097152 | tf_op jit(solution)/shard_map/all_to_all | solution.py:358
  88.9 1.0 %copy.29 = f32[1,4,1,16,4096]{4,3,2,1,0:T(8,128)} copy(f32[1,4,1,16,4096]{4,3,2,1,0:T(8,128)S(1)} %bitcast.42) | data formatting | bytes 2097152
  (1 shorter events, 0.0 us)
Async XLA Ops:
  3.7 5.3 %copy-start.5 = (s32[3,1]{0,1:T(1,128)S(1)}, s32[3,1]{0,1:T(1,128)}, u32[]{:S(2)}) copy-start(s32[3,1]{0,1:T(1,128)} %param.10) | copy-start | bytes 40
  3.7 7.9 %copy-start.4 = (f32[32,32,32]{2,1,0:T(8,128)S(1)}, f32[32,32,32]{2,1,0:T(8,128)}, u32[]{:S(2)}) copy-start(f32[32,32,32]{2,1,0:T(8,128)} %param.11) | copy-start | bytes 393220
  3.7 31.9 %all-to-all-start = ((f32[8,16,4096]{2,1,0:T(8,128)}), f32[8,16,4096]{2,1,0:T(8,128)S(1)}, u32[]{:S(2)}, u32[]{:S(2)}) async-start(f32[8,16,4096]{2,1,0:T(8,128)} %pad_maximum_fusion), calls=%async_computation | async-start | bytes 4194304 | tf_op jit(solution)/shard_map/all_to_all | solution.py:323
  11.8 23.8 %copy-start = (bf16[4,256,256]{2,1,0:T(8,128)(2,1)S(1)}, bf16[4,256,256]{2,1,0:T(8,128)(2,1)}, u32[]{:S(2)}) copy-start(bf16[4,256,256]{2,1,0:T(8,128)(2,1)} %constant.41.clone.back_rest) | copy-start | bytes 1572868
  11.8 23.8 %copy-start.1 = (bf16[4,256,256]{2,1,0:T(8,128)(2,1)S(1)}, bf16[4,256,256]{2,1,0:T(8,128)(2,1)}, u32[]{:S(2)}) copy-start(bf16[4,256,256]{2,1,0:T(8,128)(2,1)} %constant.40.clone.back_high) | copy-start | bytes 1572868
  35.7 1.0 %copy-start.2 = (bf16[4,256,256]{2,1,0:T(8,128)(2,1)S(1)}, bf16[4,256,256]{2,1,0:T(8,128)(2,1)}, u32[]{:S(2)}) copy-start(bf16[4,256,256]{2,1,0:T(8,128)(2,1)} %constant.39.clone.fwd_rest) | copy-start | bytes 1572868
  36.7 1.0 %copy-start.3 = (bf16[4,256,256]{2,1,0:T(8,128)(2,1)S(1)}, bf16[4,256,256]{2,1,0:T(8,128)(2,1)}, u32[]{:S(2)}) copy-start(bf16[4,256,256]{2,1,0:T(8,128)(2,1)} %constant.38.clone.fwd_high) | copy-start | bytes 1572868

commit v2 on v1

v2 whole, which is shorter than its diff:
```python
import functools
import math

import jax
import jax.numpy as jnp
import numpy as np
from jax import lax
from jax.experimental import pallas as pl
from jax.experimental.pallas import tpu as pltpu
from jax.sharding import PartitionSpec as P

ITERS = 4
LANES = 128
RADIX = 8
PAIRS = 4
RESIDUES = ((0, 4), (1, 7), (2, 6), (3, 5))
HALF_ROOT = math.sqrt(0.5)
ROW_BETA = 8
ROW_NORM = 16
ROW_INVERSE = 17
ROWS = 24


def cas(angle):
    return np.cos(angle) + np.sin(angle)


@functools.cache
def pair_weights(size):
    low = size // RADIX
    cells = np.arange(size)
    over_z = cas(2 * np.pi * np.outer(cells, cells) / size)
    weights = np.zeros((PAIRS, 2, low, size, 2, low, size))
    for pair, residues in enumerate(RESIDUES):
        for out_half, residue in enumerate(residues):
            for v0 in range(low):
                for y0 in range(low):
                    angle = 2 * np.pi * (residue + RADIX * v0) * y0 / size
                    cosine, sine = np.cos(angle), np.sin(angle)
                    if pair == 0:
                        weights[pair, out_half, y0, :, out_half, v0] = (cosine + sine) * over_z
                    else:
                        sign = 1.0 if out_half == 0 else -1.0
                        weights[pair, 0, y0, :, out_half, v0] = (cosine + sine) * over_z
                        weights[pair, 1, y0, :, out_half, v0] = sign * (cosine - sine) * over_z
    return weights.reshape(PAIRS, 2 * low * size, 2 * low * size)


def split_weights(weights):
    high = weights.astype(np.float32).astype(jnp.bfloat16)
    rest = (weights - high.astype(np.float64)).astype(np.float32).astype(jnp.bfloat16)
    return high, rest


def hartley(values):
    count = len(values)
    if count == 2:
        return [values[0] + values[1], values[0] - values[1]]
    even, odd = hartley(values[0::2]), hartley(values[1::2])
    half = count // 2
    first, second = [], []
    for u in range(half):
        angle = 2 * math.pi * u / count
        if u == 0:
            turned = odd[0]
        elif 4 * u == count:
            turned = odd[u]
        elif 8 * u == count:
            turned = (odd[u] + odd[half - u]) * HALF_ROOT
        elif 8 * u == 3 * count:
            turned = (odd[half - u] - odd[u]) * HALF_ROOT
        else:
            turned = odd[u] * math.cos(angle) + odd[half - u] * math.sin(angle)
        first.append(even[u] + turned)
        second.append(even[u] - turned)
    return first + second


def butterflies(f):
    a = [f[i] + f[i + 4] for i in range(4)]
    b = [f[i] - f[i + 4] for i in range(4)]
    even, odd = a[0] + a[2], a[1] + a[3]
    less, more = (b[1] - b[3]) * HALF_ROOT, (b[1] + b[3]) * HALF_ROOT
    return (
        (even + odd, even - odd),
        (b[0] + less, b[2] + more),
        (a[0] - a[2], a[1] - a[3]),
        (b[0] - less, more - b[2]),
    )


def butterflies_back(pairs):
    (c0, c4), (c1, s1), (c2, s2), (c3, s3) = pairs
    even, odd = c0 + c4, c0 - c4
    less, more = (c1 - c3) * HALF_ROOT, (s1 + s3) * HALF_ROOT
    a = [even + c2, odd + s2, even - c2, odd - s2]
    b = [c1 + c3, less + more, s1 - s3, more - less]
    return [a[i] + b[i] for i in range(4)] + [a[i] - b[i] for i in range(4)]


def total(block):
    return jnp.sum(jnp.sum(block, axis=0, keepdims=True), axis=1, keepdims=True)


def matmul3(value, high_ref, rest_ref, pair, contract):
    high = value.astype(jnp.bfloat16)
    rest = (value - high.astype(jnp.float32)).astype(jnp.bfloat16)
    dot = functools.partial(
        lax.dot_general,
        dimension_numbers=(((1,), (contract,)), ((), ())),
        preferred_element_type=jnp.float32,
    )
    return dot(high, high_ref[pair]) + (dot(rest, high_ref[pair]) + dot(high, rest_ref[pair]))


class Layout:
    def __init__(self, size, ref):
        self.groups, self.fields, width = ref.shape
        self.size = size
        self.planes = width // (size * size)

    def place(self, group, plane, block):
        start = (plane * RADIX + block) * LANES
        return group, slice(None), slice(start, start + LANES)

    def rows(self, group, plane):
        return pl.ds(pl.multiple_of((group * self.planes + plane) * self.fields, 8), self.fields)

    def over_planes(self, step, *sums):
        zero = jnp.zeros((self.fields, LANES), jnp.float32)

        def run(group, carry):
            for plane in range(self.planes):
                carry = step(group, plane, carry)
            return carry

        return [total(part) for part in lax.fori_loop(0, self.groups, run, (zero,) * len(sums))]

    def spread(self, left, group, plane, values):
        for pair, halves in enumerate(butterflies(values)):
            for half, value in enumerate(halves):
                left[pair, self.rows(group, plane), half * LANES : (half + 1) * LANES] = value

    def collect(self, right, group, plane):
        rows = self.rows(group, plane)
        return butterflies_back(
            [
                [right[pair, rows, half * LANES : (half + 1) * LANES] for half in range(2)]
                for pair in range(PAIRS)
            ]
        )

    def middle(self, left, right, pot_ref, high_ref, rest_ref):
        size, fields = self.size, self.fields

        def into(pair):
            right[pair] = matmul3(left[pair], high_ref, rest_ref, pair, 0)

        def weigh(pair):
            for half in range(2):
                lanes = slice(half * LANES, (half + 1) * LANES)
                column = [right[pair, x * fields : (x + 1) * fields, lanes] for x in range(size)]
                column = hartley(column)
                column = [column[x] * pot_ref[pair, x : x + 1, lanes] for x in range(size)]
                column = hartley(column)
                for x in range(size):
                    left[pair, x * fields : (x + 1) * fields, lanes] = column[x]

        def out(pair):
            right[pair] = matmul3(left[pair], high_ref, rest_ref, pair, 1)

        for stage in range(PAIRS + 2):
            if stage < PAIRS:
                into(stage)
            if 0 <= stage - 2:
                out(stage - 2)
            if 0 <= stage - 1 < PAIRS:
                weigh(stage - 1)


def tree_sum(values):
    while len(values) > 1:
        values = [sum(values[i : i + 2]) for i in range(0, len(values), 2)]
    return values[0]


def inverse_of(value):
    positive = value > 0.0
    return jnp.where(positive, 1.0 / jnp.where(positive, value, 1.0), 0.0)


def first_kernel(
    size, start_ref, pot_ref, high_ref, rest_ref, direct_ref, square_ref, left, right
):
    layout = Layout(size, start_ref)

    def forward(group, plane, carry):
        values = [start_ref[layout.place(group, plane, block)] for block in range(RADIX)]
        layout.spread(left, group, plane, values)
        return (carry[0] + tree_sum([value * value for value in values]),)

    (square,) = layout.over_planes(forward, 0)
    square_ref[...] = jnp.broadcast_to(square, square_ref.shape)
    layout.middle(left, right, pot_ref, high_ref, rest_ref)

    def backward(group, plane, carry):
        for block, direct in enumerate(layout.collect(right, group, plane)):
            direct_ref[layout.place(group, plane, block)] = direct
        return carry

    layout.over_planes(backward)


def recur_kernel(
    size, start_ref, direct_ref, square_ref, energy_ref, pot_ref, high_ref, rest_ref,
    basis_1, basis_2, basis_3, basis_4, message_ref, own_ref, left, right,
):
    layout = Layout(size, start_ref)
    basis = [start_ref, basis_1, basis_2, basis_3, basis_4]
    squares = [square_ref[0:1, 0:1]]
    alphas, betas, lengths = [], [], []

    def remainder(step, group, plane):
        places = [layout.place(group, plane, block) for block in range(RADIX)]
        alpha, scale = alphas[step - 1], inverse_of(lengths[step - 1])
        applied = [basis[step][place] for place in places]
        before = [basis[step - 1][place] for place in places]
        values = [(new - alpha * old) * scale for new, old in zip(applied, before)]
        for place, value in zip(places, values):
            basis[step][place] = value
        return values, tree_sum([value * value for value in values])

    for step in range(ITERS):
        if step > 0:

            def forward(group, plane, carry, step=step):
                values, part = remainder(step, group, plane)
                layout.spread(left, group, plane, values)
                return (carry[0] + part,)

            squares += layout.over_planes(forward, 0)
            layout.middle(left, right, pot_ref, high_ref, rest_ref)
            back = squares[step] * inverse_of(squares[step - 1]) * lengths[step - 1]

        def backward(group, plane, carry, step=step):
            places = [layout.place(group, plane, block) for block in range(RADIX)]
            if step == 0:
                directs = [direct_ref[place] for place in places]
            else:
                olds = [basis[step - 1][place] for place in places]
                directs = layout.collect(right, group, plane)
                directs = [direct + back * old for direct, old in zip(directs, olds)]
            values = [basis[step][place] for place in places]
            applied = [
                energy_ref[place] * value - direct
                for place, value, direct in zip(places, values, directs)
            ]
            for place, new in zip(places, applied):
                basis[step + 1][place] = new
            return (
                carry[0] + tree_sum([value * new for value, new in zip(values, applied)]),
                carry[1] + tree_sum([new * new for new in applied]),
            )

        along, whole = layout.over_planes(backward, 0, 0)
        inverse = inverse_of(squares[step])
        alpha, whole = along * inverse, whole * inverse
        alphas.append(alpha)
        lengths.append(jnp.sqrt(jnp.maximum(whole - alpha * alpha, 1e-6 * whole)))

    def last(group, plane, carry):
        return (carry[0] + remainder(ITERS, group, plane)[1],)

    squares += layout.over_planes(last, 0)
    for step in range(ITERS):
        ratio = squares[step + 1] * inverse_of(squares[step])
        betas.append(jnp.sqrt(ratio) * lengths[step])
    norms = [jnp.sqrt(square) for square in squares]
    table = {ROW_NORM: norms[0]}
    for step in range(ITERS):
        table[step], table[ROW_BETA + step] = alphas[step], betas[step]
    lane = lax.broadcasted_iota(jnp.int32, (1, LANES), 1)
    message = jnp.zeros((1, LANES), jnp.float32)
    for place, value in table.items():
        message = jnp.where(lane == place, value, message)
    message_ref[...] = jnp.broadcast_to(message[None], message_ref.shape)
    for step in range(ITERS + 1):
        table[ROW_INVERSE + step] = inverse_of(norms[step])
    row = lax.broadcasted_iota(jnp.int32, (ROWS, LANES), 0)
    own = jnp.zeros((ROWS, LANES), jnp.float32)
    for place, value in table.items():
        own = jnp.where(row == place, value, own)
    own_ref[...] = own


def combine_kernel(
    root_count, all_ref, own_ref, basis_0, basis_1, basis_2, basis_3, basis_4,
    result_ref, alpha_ref, beta_ref,
):
    basis = [basis_0, basis_1, basis_2, basis_3, basis_4]
    groups, fields, width = result_ref.shape
    table = jnp.transpose(all_ref[:, 0, :])
    wide_alpha, wide_beta = table[0:8], table[8:16]
    own_alpha, own_beta = own_ref[0:8], own_ref[8:16]
    norms = table[ROW_NORM : ROW_NORM + 1]
    inverse = 1.0 / jnp.sqrt(total(norms * norms))

    def first(norm, like):
        row = lax.broadcasted_iota(jnp.int32, like.shape, 0)
        return jnp.where(row == 0, norm * inverse, 0.0)

    def apply(diagonal, side, vector):
        return diagonal * vector + side * pltpu.roll(vector, 7, 0) + pltpu.roll(side * vector, 1, 0)

    wide = first(norms, wide_alpha)
    own = first(own_ref[ROW_NORM : ROW_NORM + 1], own_alpha)
    wide_prev, own_prev = jnp.zeros_like(wide), jnp.zeros_like(own)
    beta = jnp.zeros((1, 1), jnp.float32)
    lane = lax.broadcasted_iota(jnp.int32, (1, LANES), 1)
    alphas = jnp.zeros((1, LANES), jnp.float32)
    betas = jnp.zeros((1, LANES), jnp.float32)
    for step in range(ITERS):
        applied = apply(wide_alpha, wide_beta, wide)
        alpha = total(wide * applied)
        remainder = applied - alpha * wide - beta * wide_prev
        own_remainder = apply(own_alpha, own_beta, own) - alpha * own - beta * own_prev
        beta = jnp.sqrt(total(remainder * remainder))
        wide_prev, own_prev = wide, own
        wide, own = remainder / beta, own_remainder / beta
        alphas = jnp.where(lane == step, alpha, alphas)
        betas = jnp.where(lane == step, beta, betas)
    alpha_ref[0] = alphas[:, :ITERS]
    beta_ref[0] = betas[:, :ITERS]
    scales = own_ref[ROW_INVERSE:ROWS]
    factors = [own[i : i + 1] * scales[i : i + 1] * root_count for i in range(ITERS + 1)]

    def run(group, carry):
        for block in range(width // LANES):
            place = (group, slice(None), slice(block * LANES, (block + 1) * LANES))
            result_ref[place] = tree_sum([basis[i][place] * factors[i] for i in range(ITERS + 1)])
        return carry

    lax.fori_loop(0, groups, run, 0)


def shift_axis(part, offset, axis_number):
    length = part.shape[axis_number]
    doubled = jnp.concatenate([part, part], axis=axis_number)
    first_index = (length - offset) % length
    return lax.dynamic_slice_in_dim(doubled, first_index, length, axis_number)


def potential_table(potential, sites):
    size = potential.shape[0]
    table = potential
    for axis in range(3):
        table = shift_axis(table, sites[axis, 0], axis)
    table = table * (1.0 / size**3)
    table = table.reshape(size, size // RADIX, RADIX, size)
    pairs = [
        jnp.concatenate([table[:, :, residue].reshape(size, -1) for residue in residues], axis=1)
        for residues in RESIDUES
    ]
    return jnp.stack(pairs)


def body(start, energies, sites, potential):
    size = potential.shape[0]
    atom_count, core_count, pol_count, band_local, kpoint_local = start.shape
    assert atom_count == 1 and pol_count == 1 and size * (size // RADIX) == LANES
    groups = lax.axis_size("grid")
    devices = groups * lax.axis_size("band")
    chain = core_count * band_local
    planes = size // groups
    fields = -(-chain // groups)
    padded = -(-fields // 8) * 8

    def by_owner(part):
        part = part.reshape(chain, kpoint_local)
        if fields * groups != chain:
            part = jnp.pad(part, ((0, fields * groups - chain), (0, 0)))
        part = part.reshape(groups, fields, kpoint_local)
        if padded != fields:
            part = jnp.pad(part, ((0, 0), (0, padded - fields), (0, 0)))
        return part

    move = functools.partial(lax.all_to_all, split_axis=0, concat_axis=0, tiled=True)
    own_start = move(by_owner(start), "grid")
    own_energies = move(by_owner(energies), "grid")
    table = potential_table(potential, sites)
    high, rest = map(jnp.asarray, split_weights(pair_weights(size)))
    vmem = pl.BlockSpec(memory_space=pltpu.VMEM)
    shape = functools.partial(jax.ShapeDtypeStruct, dtype=jnp.float32)
    vector = shape((groups, padded, kpoint_local))
    scratch = pltpu.VMEM((PAIRS, size * padded, 2 * LANES), jnp.float32)

    def call(kernel, name, inputs, outputs, scratches, limit):
        return pl.pallas_call(
            kernel,
            out_shape=outputs,
            in_specs=[vmem] * len(inputs),
            out_specs=(vmem,) * len(outputs),
            scratch_shapes=scratches,
            compiler_params=pltpu.CompilerParams(vmem_limit_bytes=limit * 2**20),
            name=name,
        )(*inputs)

    direct, square = call(
        functools.partial(first_kernel, size),
        "first",
        (own_start, table, high, rest),
        (vector, shape((8, LANES))),
        [scratch] * 2,
        16,
    )
    *basis, message, own = call(
        functools.partial(recur_kernel, size),
        "recur",
        (own_start, direct, square, own_energies, table, high, rest),
        (vector,) * ITERS + (shape((devices, 1, LANES)), shape((ROWS, LANES))),
        [scratch] * 2,
        20,
    )
    gathered = move(message, ("grid", "band"))
    count = chain * lax.axis_size("band") * kpoint_local * groups
    result, alphas, betas = call(
        functools.partial(combine_kernel, math.sqrt(count)),
        "combine",
        (gathered, own, own_start, *basis),
        (vector, shape((1, 1, ITERS)), shape((1, 1, ITERS))),
        [],
        16,
    )
    back = move(result, "grid")
    back = back[:, :fields].reshape(groups * fields, kpoint_local)[:chain]
    return alphas, betas, back.reshape(start.shape)


def solution(mesh):
    in_specs = (P(None, None, None, "band", "grid"), P(None, "band", "grid"), P(), P())
    out_specs = (P(), P(), P(None, None, None, "band", "grid"))
    return jax.shard_map(body, mesh=mesh, in_specs=in_specs, out_specs=out_specs, check_vma=False)
```

time: 90.5 us -> 81.8 us (0.904)
  Pallas kernels: 22.4 us -> 12.1 us
  starting transfers between devices: 5.33 us -> 8.9 us
  waiting for transfers between devices: 17.2 us -> 20.6 us
  other arithmetic: 5.23 us -> 2.16 us
  local copies, waits for them, and re-layouts: 8.28 us -> 6.07 us
    pallas_call x2 -> x3, Pallas kernels: 22.4 us -> 12.1 us  [call(): pl.pallas_call(kernel, out_shape=outputs, in_specs=[vmem] * len(inputs),...]
    all_to_all x1 -> x2, starting transfers between devices: 5.33 us -> 8.9 us  [the longest x1 5.21 us: body(): own_start = move(by_owner(start), 'grid')]
    all_to_all x1 -> x2, waiting for transfers between devices: 17.2 us -> 20.6 us  [the longest x1 12.8 us: body(): own_start = move(by_owner(start), 'grid')]
    concatenate x1 -> x0, other arithmetic: 3.07 us -> none  [body(): both = jnp.concatenate([by_owner(start), by_owner(energies)], axis=1)]
    another operation x8, local copies, waits for them, and re-layouts: 3.63 us -> 1.95 us  [potential_table(): table[:, :, residue].reshape(size, -1)]
  transfers between devices with their start and end apart: 1 -> 2, of which waited for: 1 -> 2; matrix products, arithmetic and copies ran while one was open for 8% -> 6% of each run, Pallas kernels for 0% -> 2%
where the time goes in v2:
time: 81.8 us; the launch traced here: 81.4 us
  blocking collectives  28.7 us (35%)
  waiting for transfers between devices  20.6 us (25%)
  Pallas kernels  12.1 us (15%)
  starting transfers between devices  8.9 us (11%)
  local copies, waits for them, and re-layouts  6.07 us (7%)
  between operations  2.76 us (3%)
  other arithmetic  2.16 us (3%)
    all_to_all x1, blocking collectives, body(): back = move(result, 'grid')  17.7 us
    all_to_all x1, waiting for transfers between devices, body(): own_start = move(by_owner(start), 'grid')  12.8 us
    pallas_call x3, Pallas kernels, call(): pl.pallas_call(kernel, out_shape=outputs, in_specs=[vmem] * len(inputs),...  12.1 us
    all_to_all x1, blocking collectives, body(): gathered = move(message, ('grid', 'band'))  11 us
    all_to_all x1, waiting for transfers between devices, body(): own_energies = move(by_owner(energies), 'grid')  7.84 us
    all_to_all x1, starting transfers between devices, body(): own_start = move(by_owner(start), 'grid')  5.21 us
    all_to_all x1, starting transfers between devices, body(): own_energies = move(by_owner(energies), 'grid')  3.69 us
    unnamed x13, local copies, waits for them, and re-layouts  3.18 us
  transfers between devices with their start and end apart: 2, of which 2 were waited for; matrix products, arithmetic and copies ran while one was open for 6% of the time, Pallas kernels for 2%

profile of v2, /device:TPU:0, one launch (start us, length us, event | category | flops | bytes accessed | tf_op | source)
XLA Modules:
  0.0 81.4 jit_solution(4844434406402941461)
XLA Ops:
  0.6 0.0 copy-start.5
  0.6 5.2 %all-to-all-start = ((f32[8,8,4096]{2,1,0:T(8,128)}), f32[8,8,4096]{2,1,0:T(8,128)S(1)}, u32[]{:S(2)}, u32[]{:S(2)}) async-start(f32[8,8,4096]{2,1,0:T(8,128)} %bitcast.43), calls=%async_computation | async-start | bytes 2097152 | tf_op jit(solution)/shard_map/all_to_all | solution.py:388
  5.9 0.0 copy-done.5
  5.9 0.6 fusion.5
  8.4 12.8 %all-to-all-done.start_ref.basis_0 = f32[8,8,4096]{2,1,0:T(8,128)S(1)} async-done(((f32[8,8,4096]{2,1,0:T(8,128)}), f32[8,8,4096]{2,1,0:T(8,128)S(1)}, u32[]{:S(2)}, u32[]{:S(2)}) %all-to-all-start) | async-done | bytes 1048608 | tf_op jit(solution)/shard_map/all_to_all | solution.py:388
  21.2 0.0 copy-start.4
  21.2 3.7 %all-to-all-start.1 = ((f32[8,8,4096]{2,1,0:T(8,128)}), f32[8,8,4096]{2,1,0:T(8,128)S(1)}, u32[]{:S(2)}, u32[]{:S(2)}) async-start(f32[8,8,4096]{2,1,0:T(8,128)} %bitcast.9), calls=%async_computation.1 | async-start | bytes 2097152 | tf_op jit(solution)/shard_map/all_to_all | solution.py:389
  24.9 0.0 copy-done.4
  24.9 0.2 fusion.1
  25.1 0.2 fusion
  25.3 0.3 fusion.3
  25.7 0.4 fusion.4
  26.0 0.7 reshape_squeeze.24
  26.7 0.0 copy-start.1
  26.7 0.1 reshape_squeeze.30
  26.8 0.0 copy-start
  26.8 0.7 reshape_squeeze.29
  27.5 0.1 reshape_squeeze.28
  27.6 0.1 reshape_squeeze.27
  27.7 0.1 reshape_squeeze.26
  27.8 0.1 reshape_squeeze.25
  27.9 0.1 reshape_squeeze.31
  28.0 0.7 maximum_bitcast_fusion
  28.7 0.7 maximum_bitcast_fusion.2
  29.5 0.0 copy-done.1
  29.5 0.0 copy-done
  29.5 1.9 %first.1 = (f32[8,8,4096]{2,1,0:T(8,128)S(1)}, f32[8,128]{1,0:T(8,128)S(1)}) custom-call(f32[8,8,4096]{2,1,0:T(8,128)S(1)} %all-to-all-done.start_ref.basis_0, f32[4,32,256]{2,1,0:T(8,128)S(1)} %pad_maximum_fusion.pot_ref, bf16[4,256,256]{2,1,0:T(8,128)(2,1)S(1)} %copy-done.1, bf16[4,256,256]{2,1,0:T(8,128)(2,1)S(1)} %copy-done), custom_call_target="tpu_custom_call" | custom-call | tf_op jit(solution)/shard_map/first/pallas_call | solution.py:398
  31.4 0.0 copy-start.2
  31.4 1.0 %copy-done.2 = f32[8,8,4096]{2,1,0:T(8,128)} copy-done((f32[8,8,4096]{2,1,0:T(8,128)}, f32[8,8,4096]{2,1,0:T(8,128)S(1)}, u32[]{:S(2)}) %copy-start.2) | copy-done | bytes 1048600
  32.4 7.8 %all-to-all-done.1.energy_ref = f32[8,8,4096]{2,1,0:T(8,128)S(1)} async-done(((f32[8,8,4096]{2,1,0:T(8,128)}), f32[8,8,4096]{2,1,0:T(8,128)S(1)}, u32[]{:S(2)}, u32[]{:S(2)}) %all-to-all-start.1) | async-done | bytes 1048608 | tf_op jit(solution)/shard_map/all_to_all | solution.py:389
  40.2 0.0 copy-start.3
  40.2 1.2 %copy-done.3 = f32[8,8,4096]{2,1,0:T(8,128)S(1)} copy-done((f32[8,8,4096]{2,1,0:T(8,128)S(1)}, f32[8,8,4096]{2,1,0:T(8,128)}, u32[]{:S(2)}) %copy-start.3) | copy-done | bytes 1048600
  41.5 8.4 %recur.1 = (f32[8,8,4096]{2,1,0:T(8,128)S(1)}, f32[8,8,4096]{2,1,0:T(8,128)S(1)}, f32[8,8,4096]{2,1,0:T(8,128)S(1)}, f32[8,8,4096]{2,1,0:T(8,128)S(1)}, f32[32,1...) custom-call(f32[8,8,4096]{2,1,0:T(8,128)S(1)} %all-to-all-done.start_ref.basis_0, f32[8,8,4096]{2,1,0:T(8,128)S(1)} %copy-done.3, ...), custom_call_target="tpu_custom_call" | custom-call | tf_op jit(solution)/shard_map/recur/pallas_call | solution.py:398
  49.9 11.0 %all_to_all.20.all_ref = f32[32,1,128]{2,1,0:T(1,128)S(1)} all-to-all(f32[32,1,128]{2,1,0:T(1,128)S(1)} %get-tuple-element.16), channel_id=1, replica_groups=mesh['grid'=8,'band'=4] {'grid','band'}, dimensions={0} | all-to-all | bytes 32768 | tf_op jit(solution)/shard_map/all_to_all | solution.py:424
  60.9 1.8 %combine.1 = (f32[8,8,4096]{2,1,0:T(8,128)S(1)}, f32[1,1,4]{2,1,0:T(1,128)}, f32[1,1,4]{2,1,0:T(1,128)}) custom-call(f32[32,1,128]{2,1,0:T(1,128)S(1)} %all_to_all.20.all_ref, f32[24,128]{1,0:T(8,128)S(1)} %get-tuple-element.17.own_ref, f32[8,8,4096]{2,1,0:T(8,128)S(1)} %all-to-all-done.start_ref.basis_0, f32[8,8,4096]{2,1,0:T(8,128)S(1)} %get-tuple-element.18.basis_1, ...), custom_call_target="tpu_custom_call" | custom-call | tf_op jit(solution)/shard_map/combine/pallas_call | solution.py:398
  62.7 17.7 %all_to_all.21 = f32[8,8,4096]{2,1,0:T(8,128)S(1)} all-to-all(f32[8,8,4096]{2,1,0:T(8,128)S(1)} %get-tuple-element.24), channel_id=1, replica_groups=mesh['grid'=8,'band'=4] {'grid'}, dimensions={0} | all-to-all | bytes 2097152 | tf_op jit(solution)/shard_map/all_to_all | solution.py:434
  80.4 1.0 %copy.27 = f32[1,4,1,16,4096]{4,3,2,1,0:T(8,128)} copy(f32[1,4,1,16,4096]{4,3,2,1,0:T(8,128)S(1)} %bitcast.42) | data formatting | bytes 2097152
  (1 shorter events, 0.0 us)
Async XLA Ops:
  0.6 5.2 %copy-start.5 = (s32[3,1]{0,1:T(1,128)S(1)}, s32[3,1]{0,1:T(1,128)}, u32[]{:S(2)}) copy-start(s32[3,1]{0,1:T(1,128)} %param.8) | copy-start | bytes 40
  0.6 20.6 %all-to-all-start = ((f32[8,8,4096]{2,1,0:T(8,128)}), f32[8,8,4096]{2,1,0:T(8,128)S(1)}, u32[]{:S(2)}, u32[]{:S(2)}) async-start(f32[8,8,4096]{2,1,0:T(8,128)} %bitcast.43), calls=%async_computation | async-start | bytes 2097152 | tf_op jit(solution)/shard_map/all_to_all | solution.py:388
  21.2 3.7 %copy-start.4 = (f32[32,32,32]{2,1,0:T(8,128)S(1)}, f32[32,32,32]{2,1,0:T(8,128)}, u32[]{:S(2)}) copy-start(f32[32,32,32]{2,1,0:T(8,128)} %param.9) | copy-start | bytes 393220
  21.2 19.0 %all-to-all-start.1 = ((f32[8,8,4096]{2,1,0:T(8,128)}), f32[8,8,4096]{2,1,0:T(8,128)S(1)}, u32[]{:S(2)}, u32[]{:S(2)}) async-start(f32[8,8,4096]{2,1,0:T(8,128)} %bitcast.9), calls=%async_computation.1 | async-start | bytes 2097152 | tf_op jit(solution)/shard_map/all_to_all | solution.py:389
  26.7 2.8 %copy-start.1 = (bf16[4,256,256]{2,1,0:T(8,128)(2,1)S(1)}, bf16[4,256,256]{2,1,0:T(8,128)(2,1)}, u32[]{:S(2)}) copy-start(bf16[4,256,256]{2,1,0:T(8,128)(2,1)} %constant.34.clone.high_ref) | copy-start | bytes 1572868
  26.8 2.7 %copy-start = (bf16[4,256,256]{2,1,0:T(8,128)(2,1)S(1)}, bf16[4,256,256]{2,1,0:T(8,128)(2,1)}, u32[]{:S(2)}) copy-start(bf16[4,256,256]{2,1,0:T(8,128)(2,1)} %constant.35.clone.rest_ref) | copy-start | bytes 1572868
  31.4 1.0 %copy-start.2 = (f32[8,8,4096]{2,1,0:T(8,128)}, f32[8,8,4096]{2,1,0:T(8,128)S(1)}, u32[]{:S(2)}) copy-start(f32[8,8,4096]{2,1,0:T(8,128)S(1)} %get-tuple-element.14.direct_ref) | copy-start | bytes 3145732
  40.2 1.2 %copy-start.3 = (f32[8,8,4096]{2,1,0:T(8,128)S(1)}, f32[8,8,4096]{2,1,0:T(8,128)}, u32[]{:S(2)}) copy-start(f32[8,8,4096]{2,1,0:T(8,128)} %copy-done.2) | copy-start | bytes 3145732

commit v3 on v2

--- a/solution.py
+++ b/solution.py
@@ -161,7 +161,8 @@
                 lanes = slice(half * LANES, (half + 1) * LANES)
                 column = [right[pair, x * fields : (x + 1) * fields, lanes] for x in range(size)]
                 column = hartley(column)
-                column = [column[x] * pot_ref[pair, x : x + 1, lanes] for x in range(size)]
+                row = RESIDUES[pair][half]
+                column = [column[x] * pot_ref[x, row : row + 1] for x in range(size)]
                 column = hartley(column)
                 for x in range(size):
                     left[pair, x * fields : (x + 1) * fields, lanes] = column[x]
@@ -189,35 +190,15 @@
     return jnp.where(positive, 1.0 / jnp.where(positive, value, 1.0), 0.0)
 
 
-def first_kernel(
-    size, start_ref, pot_ref, high_ref, rest_ref, direct_ref, square_ref, left, right
-):
-    layout = Layout(size, start_ref)
-
-    def forward(group, plane, carry):
-        values = [start_ref[layout.place(group, plane, block)] for block in range(RADIX)]
-        layout.spread(left, group, plane, values)
-        return (carry[0] + tree_sum([value * value for value in values]),)
-
-    (square,) = layout.over_planes(forward, 0)
-    square_ref[...] = jnp.broadcast_to(square, square_ref.shape)
-    layout.middle(left, right, pot_ref, high_ref, rest_ref)
-
-    def backward(group, plane, carry):
-        for block, direct in enumerate(layout.collect(right, group, plane)):
-            direct_ref[layout.place(group, plane, block)] = direct
-        return carry
-
-    layout.over_planes(backward)
-
-
 def recur_kernel(
-    size, start_ref, direct_ref, square_ref, energy_ref, pot_ref, high_ref, rest_ref,
+    size, both_ref, pot_ref, high_ref, rest_ref,
     basis_1, basis_2, basis_3, basis_4, message_ref, own_ref, left, right,
 ):
-    layout = Layout(size, start_ref)
-    basis = [start_ref, basis_1, basis_2, basis_3, basis_4]
-    squares = [square_ref[0:1, 0:1]]
+    layout = Layout(size, basis_1)
+    fields = layout.fields
+    basis = [both_ref.at[:, :fields], basis_1, basis_2, basis_3, basis_4]
+    energy_ref = both_ref.at[:, fields:]
+    squares = []
     alphas, betas, lengths = [], [], []
 
     def remainder(step, group, plane):
@@ -231,24 +212,26 @@
         return values, tree_sum([value * value for value in values])
 
     for step in range(ITERS):
+
+        def forward(group, plane, carry, step=step):
+            if step == 0:
+                values = [basis[0][layout.place(group, plane, block)] for block in range(RADIX)]
+                part = tree_sum([value * value for value in values])
+            else:
+                values, part = remainder(step, group, plane)
+            layout.spread(left, group, plane, values)
+            return (carry[0] + part,)
+
+        squares += layout.over_planes(forward, 0)
+        layout.middle(left, right, pot_ref, high_ref, rest_ref)
         if step > 0:
-
-            def forward(group, plane, carry, step=step):
-                values, part = remainder(step, group, plane)
-                layout.spread(left, group, plane, values)
-                return (carry[0] + part,)
-
-            squares += layout.over_planes(forward, 0)
-            layout.middle(left, right, pot_ref, high_ref, rest_ref)
             back = squares[step] * inverse_of(squares[step - 1]) * lengths[step - 1]
 
         def backward(group, plane, carry, step=step):
             places = [layout.place(group, plane, block) for block in range(RADIX)]
-            if step == 0:
-                directs = [direct_ref[place] for place in places]
-            else:
+            directs = layout.collect(right, group, plane)
+            if step > 0:
                 olds = [basis[step - 1][place] for place in places]
-                directs = layout.collect(right, group, plane)
                 directs = [direct + back * old for direct, old in zip(directs, olds)]
             values = [basis[step][place] for place in places]
             applied = [
@@ -294,11 +277,11 @@
 
 
 def combine_kernel(
-    root_count, all_ref, own_ref, basis_0, basis_1, basis_2, basis_3, basis_4,
+    root_count, all_ref, own_ref, both_ref, basis_1, basis_2, basis_3, basis_4,
     result_ref, alpha_ref, beta_ref,
 ):
-    basis = [basis_0, basis_1, basis_2, basis_3, basis_4]
     groups, fields, width = result_ref.shape
+    basis = [both_ref.at[:, :fields], basis_1, basis_2, basis_3, basis_4]
     table = jnp.transpose(all_ref[:, 0, :])
     wide_alpha, wide_beta = table[0:8], table[8:16]
     own_alpha, own_beta = own_ref[0:8], own_ref[8:16]
@@ -357,11 +340,7 @@
         table = shift_axis(table, sites[axis, 0], axis)
     table = table * (1.0 / size**3)
     table = table.reshape(size, size // RADIX, RADIX, size)
-    pairs = [
-        jnp.concatenate([table[:, :, residue].reshape(size, -1) for residue in residues], axis=1)
-        for residues in RESIDUES
-    ]
-    return jnp.stack(pairs)
+    return table.transpose(0, 2, 1, 3).reshape(size, RADIX, LANES)
 
 
 def body(start, energies, sites, potential):
@@ -385,8 +364,7 @@
         return part
 
     move = functools.partial(lax.all_to_all, split_axis=0, concat_axis=0, tiled=True)
-    own_start = move(by_owner(start), "grid")
-    own_energies = move(by_owner(energies), "grid")
+    both = move(jnp.concatenate([by_owner(start), by_owner(energies)], axis=1), "grid")
     table = potential_table(potential, sites)
     high, rest = map(jnp.asarray, split_weights(pair_weights(size)))
     vmem = pl.BlockSpec(memory_space=pltpu.VMEM)
@@ -405,18 +383,10 @@
             name=name,
         )(*inputs)
 
-    direct, square = call(
-        functools.partial(first_kernel, size),
-        "first",
-        (own_start, table, high, rest),
-        (vector, shape((8, LANES))),
-        [scratch] * 2,
-        16,
-    )
     *basis, message, own = call(
         functools.partial(recur_kernel, size),
         "recur",
-        (own_start, direct, square, own_energies, table, high, rest),
+        (both, table, high, rest),
         (vector,) * ITERS + (shape((devices, 1, LANES)), shape((ROWS, LANES))),
         [scratch] * 2,
         20,
@@ -426,7 +396,7 @@
     result, alphas, betas = call(
         functools.partial(combine_kernel, math.sqrt(count)),
         "combine",
-        (gathered, own, own_start, *basis),
+        (gathered, own, both, *basis),
         (vector, shape((1, 1, ITERS)), shape((1, 1, ITERS))),
         [],
         16,

time: 81.8 us -> 77.4 us (0.946)
  starting transfers between devices: 8.9 us -> 5.33 us
  local copies, waits for them, and re-layouts: 6.07 us -> 3.8 us
  other arithmetic: 2.16 us -> 3.79 us
    all_to_all x2 -> x1, starting transfers between devices: 8.9 us -> 5.33 us  [body(): move(jnp.concatenate([by_owner(start), by_owner(energies)], axis=1), 'grid')]
    concatenate x0 -> x1, other arithmetic: none -> 3.09 us  [body(): jnp.concatenate([by_owner(start), by_owner(energies)], axis=1)]
    reshape x0 -> x2, local copies, waits for them, and re-layouts: none -> 2.22 us  [the longest x1 1.29 us: potential_table(): return table.transpose(0, 2, 1, 3).reshape(size, RADIX, LANES)]
    unnamed x13 -> x9, local copies, waits for them, and re-layouts: 3.18 us -> 0.99 us
    another operation x8 -> x0, local copies, waits for them, and re-layouts: 1.95 us -> none  [potential_table(): table[:, :, residue].reshape(size, -1)]
    another operation x3 -> x0, other arithmetic: 1.46 us -> none  [potential_table(): return jnp.stack(pairs)]
    pallas_call x3 -> x2, Pallas kernels: 12.1 us -> 11.6 us  [call(): pl.pallas_call(kernel, out_shape=outputs, in_specs=[vmem] * len(inputs),...]
    all_to_all x2 -> x1, waiting for transfers between devices: 20.6 us -> 21 us  [body(): move(jnp.concatenate([by_owner(start), by_owner(energies)], axis=1), 'grid')]
  transfers between devices with their start and end apart: 2 -> 1, of which waited for: 2 -> 1; matrix products, arithmetic and copies ran while one was open for 6% -> 5% of each run, Pallas kernels for 2% -> 0%
where the time goes in v3:
time: 77.4 us; the launch traced here: 77 us
  blocking collectives  28.8 us (37%)
  waiting for transfers between devices  21 us (27%)
  Pallas kernels  11.6 us (15%)
  starting transfers between devices  5.33 us (7%)
  local copies, waits for them, and re-layouts  3.8 us (5%)
  other arithmetic  3.79 us (5%)
  between operations  2.7 us (3%)
    all_to_all x1, waiting for transfers between devices, body(): move(jnp.concatenate([by_owner(start), by_owner(energies)], axis=1), 'grid')  21 us
    all_to_all x1, blocking collectives, body(): back = move(result, 'grid')  17.7 us
    pallas_call x2, Pallas kernels, call(): pl.pallas_call(kernel, out_shape=outputs, in_specs=[vmem] * len(inputs),...  11.6 us
    all_to_all x1, blocking collectives, body(): gathered = move(message, ('grid', 'band'))  11 us
    all_to_all x1, starting transfers between devices, body(): move(jnp.concatenate([by_owner(start), by_owner(energies)], axis=1), 'grid')  5.33 us
    concatenate x1, other arithmetic, body(): jnp.concatenate([by_owner(start), by_owner(energies)], axis=1)  3.09 us
  transfers between devices with their start and end apart: 1, of which 1 were waited for; matrix products, arithmetic and copies ran while one was open for 5% of the time, Pallas kernels for 0%

profile of v3, /device:TPU:0, one launch (start us, length us, event | category | flops | bytes accessed | tf_op | source)
XLA Modules:
  0.0 77.0 jit_solution(11915518194660109813)
XLA Ops:
  0.6 3.1 %pad_maximum_fusion = f32[8,16,4096]{2,1,0:T(8,128)} fusion(f32[8,8,4096]{2,1,0:T(8,128)} %bitcast.15, f32[8,8,4096]{2,1,0:T(8,128)} %bitcast.16), kind=kLoop, calls=%fused_computation | loop fusion | flops 524288 | bytes 4194304 | tf_op jit(solution)/shard_map/concatenate | solution.py:367
  3.7 0.0 copy-start.3
  3.7 0.0 copy-start.2
  3.7 5.3 %all-to-all-start = ((f32[8,16,4096]{2,1,0:T(8,128)}), f32[8,16,4096]{2,1,0:T(8,128)S(1)}, u32[]{:S(2)}, u32[]{:S(2)}) async-start(f32[8,16,4096]{2,1,0:T(8,128)} %pad_maximum_fusion), calls=%async_computation | async-start | bytes 4194304 | tf_op jit(solution)/shard_map/all_to_all | solution.py:367
  9.1 0.0 copy-done.3
  9.1 0.6 fusion.4
  11.7 0.0 copy-done.2
  11.7 0.2 fusion.1
  11.8 0.0 copy-start
  11.9 0.0 copy-start.1
  11.9 0.2 fusion
  12.1 0.3 fusion.3
  12.4 0.9 %copy.12 = f32[32,4,8,32]{3,1,2,0:T(4,128)} copy(f32[32,4,8,32]{3,2,1,0:T(8,128)S(1)} %fusion.3) | data formatting | bytes 262144 | tf_op jit(solution)/shard_map/reshape | solution.py:342
  13.3 1.3 %reshape.19.pot_ref = f32[32,8,128]{2,1,0:T(8,128)S(1)} reshape(f32[32,8,4,32]{3,2,1,0:T(4,128)} %bitcast.14) | data formatting | bytes 262144 | tf_op jit(solution)/shard_map/reshape | solution.py:343
  14.6 21.0 %all-to-all-done.both_ref = f32[8,16,4096]{2,1,0:T(8,128)S(1)} async-done(((f32[8,16,4096]{2,1,0:T(8,128)}), f32[8,16,4096]{2,1,0:T(8,128)S(1)}, u32[]{:S(2)}, u32[]{:S(2)}) %all-to-all-start) | async-done | bytes 2097184 | tf_op jit(solution)/shard_map/all_to_all | solution.py:367
  35.7 0.0 copy-done
  35.7 0.0 copy-done.1
  35.7 9.9 %recur.1 = (f32[8,8,4096]{2,1,0:T(8,128)S(1)}, f32[8,8,4096]{2,1,0:T(8,128)S(1)}, f32[8,8,4096]{2,1,0:T(8,128)S(1)}, f32[8,8,4096]{2,1,0:T(8,128)S(1)}, f32[32,1...) custom-call(f32[8,16,4096]{2,1,0:T(8,128)S(1)} %all-to-all-done.both_ref, f32[32,8,128]{2,1,0:T(8,128)S(1)} %reshape.19.pot_ref, ...), custom_call_target="tpu_custom_call" | custom-call | tf_op jit(solution)/shard_map/recur/pallas_call | solution.py:376
  45.5 11.0 %all_to_all.15.all_ref = f32[32,1,128]{2,1,0:T(1,128)S(1)} all-to-all(f32[32,1,128]{2,1,0:T(1,128)S(1)} %get-tuple-element.12), channel_id=1, replica_groups=mesh['grid'=8,'band'=4] {'grid','band'}, dimensions={0} | all-to-all | bytes 32768 | tf_op jit(solution)/shard_map/all_to_all | solution.py:394
  56.6 1.8 %combine.1 = (f32[8,8,4096]{2,1,0:T(8,128)S(1)}, f32[1,1,4]{2,1,0:T(1,128)}, f32[1,1,4]{2,1,0:T(1,128)}) custom-call(f32[32,1,128]{2,1,0:T(1,128)S(1)} %all_to_all.15.all_ref, f32[24,128]{1,0:T(8,128)S(1)} %get-tuple-element.13.own_ref, f32[8,16,4096]{2,1,0:T(8,128)S(1)} %all-to-all-done.both_ref, f32[8,8,4096]{2,1,0:T(8,128)S(1)} %get-tuple-element.14.basis_1, ...), custom_call_target="tpu_custom_call" | custom-call | tf_op jit(solution)/shard_map/combine/pallas_call | solution.py:376
  58.3 17.7 %all_to_all.16 = f32[8,8,4096]{2,1,0:T(8,128)S(1)} all-to-all(f32[8,8,4096]{2,1,0:T(8,128)S(1)} %get-tuple-element.20), channel_id=1, replica_groups=mesh['grid'=8,'band'=4] {'grid'}, dimensions={0} | all-to-all | bytes 2097152 | tf_op jit(solution)/shard_map/all_to_all | solution.py:404
  76.0 1.0 %copy.14 = f32[1,4,1,16,4096]{4,3,2,1,0:T(8,128)} copy(f32[1,4,1,16,4096]{4,3,2,1,0:T(8,128)S(1)} %bitcast.13) | data formatting | bytes 2097152
Async XLA Ops:
  3.7 5.3 %copy-start.3 = (s32[3,1]{0,1:T(1,128)S(1)}, s32[3,1]{0,1:T(1,128)}, u32[]{:S(2)}) copy-start(s32[3,1]{0,1:T(1,128)} %param.8) | copy-start | bytes 40
  3.7 7.9 %copy-start.2 = (f32[32,32,32]{2,1,0:T(8,128)S(1)}, f32[32,32,32]{2,1,0:T(8,128)}, u32[]{:S(2)}) copy-start(f32[32,32,32]{2,1,0:T(8,128)} %param.9) | copy-start | bytes 393220
  3.7 31.9 %all-to-all-start = ((f32[8,16,4096]{2,1,0:T(8,128)}), f32[8,16,4096]{2,1,0:T(8,128)S(1)}, u32[]{:S(2)}, u32[]{:S(2)}) async-start(f32[8,16,4096]{2,1,0:T(8,128)} %pad_maximum_fusion), calls=%async_computation | async-start | bytes 4194304 | tf_op jit(solution)/shard_map/all_to_all | solution.py:367
  11.8 23.8 %copy-start = (bf16[4,256,256]{2,1,0:T(8,128)(2,1)S(1)}, bf16[4,256,256]{2,1,0:T(8,128)(2,1)}, u32[]{:S(2)}) copy-start(bf16[4,256,256]{2,1,0:T(8,128)(2,1)} %constant.35.clone.rest_ref) | copy-start | bytes 1572868
  11.9 23.8 %copy-start.1 = (bf16[4,256,256]{2,1,0:T(8,128)(2,1)S(1)}, bf16[4,256,256]{2,1,0:T(8,128)(2,1)}, u32[]{:S(2)}) copy-start(bf16[4,256,256]{2,1,0:T(8,128)(2,1)} %constant.34.clone.high_ref) | copy-start | bytes 1572868
